TPU v7x, 32 devices: a whole 2x2x4 slice. The times are simulated.
32 devices in a mesh: grp: 4 (over z), blk: 8 (over y, x, core).
Axes of the slice: x: 2, y: 2, z: 4, core: 2. Of those that a mesh axis runs over, the one named last changes fastest.
Arguments:
- partials: bfloat16 [4, 512, 3584], P('grp', 'blk'), may hold values from -450 to 450
- slot_of_block: int32 [7], replicated, may hold values from 0 to 7, as said below
- stat_left: float32 [8, 512, 512], P('blk'), may hold values from -1 to 257, as said below
- stat_right: float32 [8, 512, 512], P('blk'), may hold values from -1 to 257, as said below
- root_left: bfloat16 [8, 512, 512], P('blk'), may hold values from -0.2 to 2.2, as said below
- root_right: bfloat16 [8, 512, 512], P('blk'), may hold values from -0.2 to 2.2, as said below
Outputs:
- new_left: float32 [8, 512, 512], P('blk')
- new_right: float32 [8, 512, 512], P('blk')
- update: bfloat16 [512, 3584], P('blk')
Inputs may be any that keep to these rules, and one draw needn't show every extreme that they name: `slot_of_block`: the 7 owners are distinct. `stat_left`: symmetric. `stat_right`: symmetric. `root_left`: symmetric. `root_right`: symmetric.
All inputs are finite; a program needn't handle non-finite values.
Results may differ from a plain program's by a relative error of at most 0.02.
Values may be sent and summed in bfloat16 or wider, within the bound.
A program may use at most 64 MiB of HBM per device.

v0:
```python
import math

import jax
import jax.numpy as jnp
from jax import lax
from jax.sharding import PartitionSpec as P

beta_two = 0.9


def shards(partials, slot_of_block, stat_left, stat_right, root_left, root_right):
    row_count = partials.shape[1]
    col_count = partials.shape[2]
    block_size = stat_left.shape[1]
    block_count = col_count // block_size
    owners = lax.axis_size("blk")
    selector = (slot_of_block[:, None] == jnp.arange(owners, dtype=jnp.int32)[None, :]).astype(
        jnp.bfloat16
    )
    summed = lax.psum(partials[0].astype(jnp.float32).astype(jnp.bfloat16), "grp")
    widened = summed.astype(jnp.float32)
    local_sq = jnp.sum(widened * widened)
    shaped = summed.reshape(row_count, block_count, block_size)
    owned_tile = lax.all_to_all(
        jnp.einsum("rbc,bs->src", shaped, selector, preferred_element_type=jnp.float32).astype(
            jnp.bfloat16
        ),
        "blk",
        split_axis=0,
        concat_axis=1,
        tiled=True,
    )[0]
    owned_wide = owned_tile.astype(jnp.float32)
    owned_sq = jnp.sum(owned_wide * owned_wide)
    squares = lax.psum(local_sq, "blk")
    norm_limit = math.sqrt(block_size * col_count)
    norm_factor = norm_limit / jnp.sqrt(squares)
    left_gram = jnp.dot(owned_tile, owned_tile.T, preferred_element_type=jnp.float32)
    right_gram = jnp.dot(owned_tile.T, owned_tile, preferred_element_type=jnp.float32)
    factor_sq = norm_factor * norm_factor
    next_left = beta_two * stat_left[0] + (1.0 - beta_two) * factor_sq * left_gram
    next_right = beta_two * stat_right[0] + (1.0 - beta_two) * factor_sq * right_gram
    halfway = jnp.dot(root_left[0], owned_tile, preferred_element_type=jnp.float32).astype(
        jnp.bfloat16
    )
    direction = jnp.dot(halfway, root_right[0], preferred_element_type=jnp.float32)
    grad_norm = jnp.sqrt(owned_sq)
    dir_norm = jnp.sqrt(jnp.sum(direction * direction) + 1e-06)
    grafted = (norm_factor * grad_norm / dir_norm * direction).astype(jnp.bfloat16)
    returned = lax.all_to_all(grafted[None], "blk", split_axis=1, concat_axis=0, tiled=True)
    update = jnp.einsum("src,bs->rbc", returned, selector, preferred_element_type=jnp.float32)
    update = update.astype(jnp.bfloat16).reshape(row_count, col_count)
    return (next_left[None], next_right[None], update)


def solution(mesh):
    return jax.shard_map(
        shards,
        mesh=mesh,
        in_specs=(
            P("grp", "blk", None),
            P(),
            P("blk", None, None),
            P("blk", None, None),
            P("blk", None, None),
            P("blk", None, None),
        ),
        out_specs=(P("blk", None, None), P("blk", None, None), P("blk", None)),
        check_vma=False,
    )
```

profile of v0, /device:TPU:0, one launch (start us, length us, event | category | flops | bytes accessed | tf_op | source)
XLA Modules:
  0.0 107.3 jit_solution(16680097260482063913)
XLA Ops:
  7.2 0.0 copy-start
  7.2 0.0 all-reduce.2.cloned.1.call-start
  7.2 0.7 all-reduce.2.cloned.1.call-update
  7.9 0.0 copy-start.3
  7.9 42.7 %all-reduce.2.cloned.1.call-done = bf16[64,3584]{1,0:T(8,128)(2,1)} async-done(((bf16[64,3584]{1,0:T(8,128)(2,1)}), bf16[64,3584]{1,0:T(8,128)(2,1)}) %all-reduce.2.cloned.1.call-update) | async-done | bytes 458768 | tf_op jit(solution)/shard_map/psum | solution.py:20
  50.6 1.6 %reshape.24 = bf16[64,7,512]{2,1,0:T(8,128)(2,1)S(1)} reshape(bf16[64,3584]{1,0:T(8,128)(2,1)} %all-reduce.2.cloned.1.call-done) | data formatting | bytes 917504 | tf_op jit(solution)/shard_map/reshape | solution.py:23
  52.2 0.0 copy-done.3
  52.2 0.4 convolution_convert_fusion.2
  52.6 0.9 copy.24
  53.6 3.8 %all-to-all-start = ((bf16[8,64,512]{2,1,0:T(8,128)(2,1)}), bf16[8,64,512]{2,1,0:T(8,128)(2,1)S(1)}, u32[]{:S(2)}, u32[]{:S(2)}) async-start(bf16[8,64,512]{2,1,0:T(8,128)(2,1)} %copy.24), calls=%async_computation | async-start | bytes 1048576 | tf_op jit(solution)/shard_map/all_to_all | solution.py:24
  57.4 0.0 copy-done.1
  57.4 0.8 multiply_reduce_fusion.2
  58.2 15.9 %psum.15 = f32[]{:T(128)} all-reduce(f32[]{:T(128)} %multiply_reduce_fusion.2), channel_id=1, replica_groups=mesh['grp'=4,'blk'=8] {'blk'}, use_global_device_ids=true, to_apply=%region_2.0 | all-reduce | flops 1 | bytes 8 | tf_op jit(solution)/shard_map/psum | solution.py:35
  74.8 0.0 all-to-all-done
  74.8 0.0 copy-done
  74.8 1.6 %multiply_reduce_fusion = (f32[]{:T(128)}, f32[512,512]{1,0:T(8,128)S(1)}) fusion(bf16[1,512,512]{2,1,0:T(8,128)(2,1)S(1)} %copy-done, bf16[512,512]{1,0:T(8,128)(2,1)S(1)} %bitcast.50, bf16[1,512,512]{2,1,0:T(8,128)(2,1)S(1)} %copy-done.5), kind=kOutput, calls=%fused_computation.12 | convolution fusion | flops 537657344 | bytes 2621444 | tf_op jit(solution)/shard_map/dot_general | solution.py:46
  77.1 0.9 multiply_reduce_fusion.1
  78.7 0.1 fusion.6
  78.8 0.8 copy.34
  79.6 0.5 broadcast.10
  80.1 3.8 %reduce.1 = bf16[512,512]{1,0:T(8,128)(2,1)S(1)} reduce(bf16[512,1,512]{2,1,0:T(2,128)(2,1)S(1)} %bitcast.53, bf16[]{:T(256)} %broadcast.10), dimensions={1}, to_apply=%bitcast.49.reduce_sub_computation | reduce | bytes 1048578
  83.9 1.2 %reshape.29 = bf16[8,2,16384]{2,1,0:T(2,128)(2,1)} reshape(bf16[512,512]{1,0:T(8,128)(2,1)S(1)} %reduce.1) | data formatting | bytes 1048576
  85.1 3.6 %all-to-all-start.1 = ((bf16[8,2,16384]{2,1,0:T(2,128)(2,1)}), bf16[8,2,16384]{2,1,0:T(2,128)(2,1)S(1)}, u32[]{:S(2)}, u32[]{:S(2)}) async-start(bf16[8,2,16384]{2,1,0:T(2,128)(2,1)} %reshape.29), calls=%async_computation.1 | async-start | bytes 1048576 | tf_op jit(solution)/shard_map/all_to_all | solution.py:50
  88.8 0.0 copy-start.4
  88.8 1.4 %fusion.4 = f32[1,512,512]{2,1,0:T(8,128)} fusion(bf16[512,512]{1,0:T(8,128)(2,1)S(1)} %bitcast.51, f32[1,512,512]{2,1,0:T(8,128)S(1)} %copy-done.2, f32[]{:T(128)S(6)} %mul.52), kind=kOutput, calls=%fused_computation.6 | convolution fusion | flops 269221888 | bytes 2621444 | tf_op jit(solution)/shard_map/dot_general | solution.py:38
  90.2 0.0 copy-done.4
  90.2 1.4 %fusion.2 = f32[1,512,512]{2,1,0:T(8,128)} fusion(bf16[8,64,512]{2,1,0:T(8,128)(2,1)S(1)} %all-to-all-done, f32[1,512,512]{2,1,0:T(8,128)S(1)} %copy-done.4, f32[]{:T(128)S(6)} %mul.52), kind=kOutput, calls=%fused_computation.3 | convolution fusion | flops 269221888 | bytes 2621444 | tf_op jit(solution)/shard_map/dot_general | solution.py:39
  91.6 6.7 %all-to-all-done.1 = bf16[8,2,16384]{2,1,0:T(2,128)(2,1)S(1)} async-done(((bf16[8,2,16384]{2,1,0:T(2,128)(2,1)}), bf16[8,2,16384]{2,1,0:T(2,128)(2,1)S(1)}, u32[]{:S(2)}, u32[]{:S(2)}) %all-to-all-start.1) | async-done | bytes 524320 | tf_op jit(solution)/shard_map/all_to_all | solution.py:50
  98.4 0.5 reshape.30
  98.9 0.1 copy.29
  99.1 0.4 convolution_convert_fusion.1
  99.5 0.9 copy.30
  (5 shorter events, 0.0 us)
Async XLA Ops:
  7.2 67.6 %copy-start = (bf16[1,512,512]{2,1,0:T(8,128)(2,1)S(1)}, bf16[1,512,512]{2,1,0:T(8,128)(2,1)}, u32[]{:S(2)}) copy-start(bf16[1,512,512]{2,1,0:T(8,128)(2,1)} %param.11) | copy-start | bytes 1572868
  7.2 43.4 %all-reduce.2.cloned.1.call-start = ((), (), s32[]{:S(2)}) async-start(), calls=%async_computation.2 | async-start | bytes 917504 | tf_op jit(solution)/shard_map/psum | solution.py:20
  7.9 44.3 %copy-start.3 = (s32[7]{0:T(128)S(1)}, s32[7]{0:T(128)}, u32[]{:S(2)}) copy-start(s32[7]{0:T(128)} %param.7) | copy-start | bytes 88
  53.6 3.8 %copy-start.1 = (bf16[64,3584]{1,0:T(8,128)(2,1)S(1)}, bf16[64,3584]{1,0:T(8,128)(2,1)}, u32[]{:S(2)}) copy-start(bf16[64,3584]{1,0:T(8,128)(2,1)} %all-reduce.2.cloned.1.call-done) | copy-start | bytes 1376260
  53.6 21.2 %copy-start.5 = (bf16[1,512,512]{2,1,0:T(8,128)(2,1)S(1)}, bf16[1,512,512]{2,1,0:T(8,128)(2,1)}, u32[]{:S(2)}) copy-start(bf16[1,512,512]{2,1,0:T(8,128)(2,1)} %param.10) | copy-start | bytes 1572868
  53.6 21.2 %all-to-all-start = ((bf16[8,64,512]{2,1,0:T(8,128)(2,1)}), bf16[8,64,512]{2,1,0:T(8,128)(2,1)S(1)}, u32[]{:S(2)}, u32[]{:S(2)}) async-start(bf16[8,64,512]{2,1,0:T(8,128)(2,1)} %copy.24), calls=%async_computation | async-start | bytes 1048576 | tf_op jit(solution)/shard_map/all_to_all | solution.py:24
  85.1 3.6 %copy-start.2 = (f32[1,512,512]{2,1,0:T(8,128)S(1)}, f32[1,512,512]{2,1,0:T(8,128)}, u32[]{:S(2)}) copy-start(f32[1,512,512]{2,1,0:T(8,128)} %param.8) | copy-start | bytes 3145732
  85.1 13.3 %all-to-all-start.1 = ((bf16[8,2,16384]{2,1,0:T(2,128)(2,1)}), bf16[8,2,16384]{2,1,0:T(2,128)(2,1)S(1)}, u32[]{:S(2)}, u32[]{:S(2)}) async-start(bf16[8,2,16384]{2,1,0:T(2,128)(2,1)} %reshape.29), calls=%async_computation.1 | async-start | bytes 1048576 | tf_op jit(solution)/shard_map/all_to_all | solution.py:50
  88.8 1.5 %copy-start.4 = (f32[1,512,512]{2,1,0:T(8,128)S(1)}, f32[1,512,512]{2,1,0:T(8,128)}, u32[]{:S(2)}) copy-start(f32[1,512,512]{2,1,0:T(8,128)} %param.9) | copy-start | bytes 3145732
Sparse Core Ops, SparseCore 0:
  10.3 40.2 all-reduce.1
where the time goes:
time: 108 us; the launch traced here: 107 us
  waiting for transfers between devices  50.1 us (46%)
  between operations  16.3 us (15%)
  blocking collectives  15.9 us (15%)
  starting transfers between devices  7.45 us (7%)
  local copies, waits for them, and re-layouts  6.6 us (6%)
  other arithmetic  5.64 us (5%)
  matrix products  5.32 us (5%)
    psum x1, waiting for transfers between devices, shards(): lax.psum(partials[0].astype(jnp.float32).astype(jnp.bfloat16), 'grp')  42.7 us
    psum x1, blocking collectives, shards(): squares = lax.psum(local_sq, 'blk')  15.9 us
    all_to_all x1, waiting for transfers between devices, shards(): lax.all_to_all(grafted[None], 'blk', split_axis=1, concat_axis=0, tiled=T...  6.74 us
    unnamed x1, other arithmetic  3.82 us
    all_to_all x1, starting transfers between devices, shards(): lax.all_to_all(jnp.einsum('rbc,bs->src', shaped, selector, preferred_elem...  3.79 us
    all_to_all x1, starting transfers between devices, shards(): lax.all_to_all(grafted[None], 'blk', split_axis=1, concat_axis=0, tiled=T...  3.62 us
    unnamed x17, local copies, waits for them, and re-layouts  3.29 us
  transfers between devices with their start and end apart: 3, of which 2 were waited for; matrix products, arithmetic and copies ran while one was open for 3% of the time, Pallas kernels for 0%

commit v1 on v0

v1 whole, which is shorter than its diff:
```python
import functools
import math

import jax
import jax.numpy as jnp
from jax import lax
from jax.experimental import pallas as pl
from jax.experimental.pallas import tpu as pltpu
from jax.sharding import PartitionSpec as P

MESH = pl.DeviceIdType.MESH
beta_two = 0.9


def partner(me, k, count):
    if count & (count - 1):
        return lax.rem(me + k, count)
    total, bit = 0, 1
    while bit < count:
        total = total + lax.rem(me // bit + k // bit, 2) * bit
        bit *= 2
    return total


def kernel(
    n_grp, n_blk, slot_ref, x_ref, sl_ref, sr_ref, rl_ref, rr_ref, nl_ref, nr_ref, up_ref,
    xb, snd, rz, tile, dirs, ret, st_out, st_in, scales, sl, sr, rl, rr,
    x_sem, w_sem, a_send, z_recv, b_send, p_send, p_recv, d_send, d_recv, s_send, s_recv,
):
    grp, blk = lax.axis_index("grp"), lax.axis_index("blk")
    n_tiles = xb.shape[0] - 1
    rows, block = xb.shape[1], xb.shape[2]
    half = n_grp // 2
    low = grp < half
    step = jnp.where(low, 1, -1)
    depth = jnp.where(low, half - 1 - grp, grp - half)
    is_mid = depth == 0
    is_end = depth == half - 1
    inner = grp + step
    outer = jnp.where(is_end, grp, grp - step)
    lag = jnp.where(is_end, n_blk, jnp.minimum(2 + 3 * depth, n_blk))

    def x_copy(b):
        cols = pl.ds(pl.multiple_of(b * block, block), block)
        return pltpu.make_async_copy(x_ref.at[0, :, cols], xb.at[b], x_sem.at[b])

    def x_start(b, c):
        x_copy(b).start()
        return c

    def x_wait(b, c):
        x_copy(b).wait()
        return c

    lax.fori_loop(0, n_tiles, x_start, 0)
    w_pairs = ((rl_ref, rl), (rr_ref, rr), (sl_ref, sl), (sr_ref, sr))
    w_copies = [
        pltpu.make_async_copy(src.at[0], dst, w_sem.at[i]) for i, (src, dst) in enumerate(w_pairs)
    ]
    for c in w_copies:
        c.start()

    barrier = pltpu.get_barrier_semaphore()

    def greet(k, c):
        pl.semaphore_signal(
            barrier, inc=1, device_id=(grp, partner(blk, k, n_blk)), device_id_type=MESH
        )
        return c

    pl.semaphore_signal(barrier, inc=1, device_id=(inner, blk), device_id_type=MESH)

    @pl.when(jnp.logical_not(is_end))
    def _():
        pl.semaphore_signal(barrier, inc=1, device_id=(outer, blk), device_id_type=MESH)

    lax.fori_loop(1, n_blk, greet, 0)
    xb[n_tiles] = jnp.zeros((rows, block), xb.dtype)
    lax.fori_loop(0, n_tiles, x_wait, 0)
    pl.semaphore_wait(barrier, n_blk + jnp.where(is_end, 0, 1))

    kind = jnp.where(is_mid, 1, 0)

    def target(t):
        return partner(blk, lax.rem(t + 1, n_blk), n_blk)

    def copy_in(s):
        return pltpu.make_async_remote_copy(
            snd.at[s], rz.at[kind, s], a_send.at[s], z_recv.at[kind, s],
            device_id=(inner, blk), device_id_type=MESH,
        )

    def copy_out(s):
        return pltpu.make_async_remote_copy(
            rz.at[1, s], rz.at[1, s], b_send.at[s], z_recv.at[1, s],
            device_id=(outer, blk), device_id_type=MESH,
        )

    def arrived(k, s):
        return pltpu.make_async_remote_copy(
            rz.at[k, s], rz.at[k, s], a_send.at[s], z_recv.at[k, s],
            device_id=(inner, blk), device_id_type=MESH,
        )

    def copy_tile(s):
        return pltpu.make_async_remote_copy(
            rz.at[1, s], tile.at[blk], p_send.at[s], p_recv.at[blk],
            device_id=(grp, s), device_id_type=MESH,
        )

    def phase(t, c):
        @pl.when(t < n_blk)
        def _():
            s = target(t)
            b = n_tiles
            for i in range(n_tiles):
                b = jnp.where(slot_ref[i] == s, i, b)

            @pl.when(is_end)
            def _():
                snd[s] = xb[b]

            @pl.when(jnp.logical_not(is_end))
            def _():
                arrived(0, s).wait_recv()
                snd[s] = (xb[b].astype(jnp.float32) + rz[0, s].astype(jnp.float32)).astype(snd.dtype)

            copy_in(s).start()

        @pl.when(jnp.logical_and(t >= lag, t < n_blk + lag))
        def _():
            s = target(t - lag)
            arrived(1, s).wait_recv()

            @pl.when(is_mid)
            def _():
                rz[1, s] = (snd[s].astype(jnp.float32) + rz[1, s].astype(jnp.float32)).astype(rz.dtype)

            @pl.when(jnp.logical_not(is_end))
            def _():
                copy_out(s).start()

            @pl.when(t - lag < n_blk - 1)
            def _():
                copy_tile(s).start()

        return c

    lax.fori_loop(0, 2 * n_blk, phase, 0)
    tile[blk] = rz[1, blk]

    def tile_wait(k, c):
        j = partner(blk, k, n_blk)
        pltpu.make_async_remote_copy(
            rz.at[1, j], tile.at[j], p_send.at[j], p_recv.at[j],
            device_id=(grp, j), device_id_type=MESH,
        ).wait_recv()
        return c

    lax.fori_loop(1, n_blk, tile_wait, 0)
    w_copies[0].wait()
    w_copies[1].wait()

    owned = tile[...].reshape(n_blk * rows, block)
    halfway = jnp.dot(rl[...], owned, preferred_element_type=jnp.float32).astype(jnp.bfloat16)
    direction = jnp.dot(halfway, rr[...], preferred_element_type=jnp.float32)
    dirs[...] = direction.astype(dirs.dtype).reshape(n_blk, rows, block)

    def copy_dir(j):
        return pltpu.make_async_remote_copy(
            dirs.at[j], ret.at[blk], d_send.at[j], d_recv.at[blk],
            device_id=(grp, j), device_id_type=MESH,
        )

    def copy_stat(j):
        return pltpu.make_async_remote_copy(
            st_out, st_in.at[blk], s_send.at[j], s_recv.at[blk],
            device_id=(grp, j), device_id_type=MESH,
        )

    wide = owned.astype(jnp.float32)
    own_sq = jnp.sum(wide * wide)
    dir_sq = jnp.sum(direction * direction)
    row_id = lax.broadcasted_iota(jnp.int32, st_out.shape, 0)
    stats = jnp.where(row_id == 0, own_sq, dir_sq)
    st_out[...] = stats
    st_in[blk] = stats

    def stat_start(k, c):
        copy_stat(partner(blk, k, n_blk)).start()
        return c

    def dir_start(k, c):
        copy_dir(partner(blk, n_blk - k, n_blk)).start()
        return c

    lax.fori_loop(1, n_blk, stat_start, 0)
    lax.fori_loop(1, n_blk, dir_start, 0)
    ret[blk] = dirs[blk]

    nl_ref[0] = lax.dot_general(
        owned, owned, (((1,), (1,)), ((), ())), preferred_element_type=jnp.float32
    )
    nr_ref[0] = lax.dot_general(
        owned, owned, (((0,), (0,)), ((), ())), preferred_element_type=jnp.float32
    )

    def stat_wait(k, c):
        j = partner(blk, k, n_blk)
        pltpu.make_async_remote_copy(
            st_out, st_in.at[j], s_send.at[j], s_recv.at[j],
            device_id=(grp, j), device_id_type=MESH,
        ).wait()
        return c

    lax.fori_loop(1, n_blk, stat_wait, 0)
    squares = jnp.zeros((1, st_out.shape[1]), jnp.float32)
    for j in range(n_blk):
        squares = squares + st_in[j, 0:1, :]
    norm_factor = math.sqrt(block * n_tiles * block) / jnp.sqrt(squares)
    for j in range(n_blk):
        scales[j] = norm_factor * jnp.sqrt(st_in[j, 0:1, :]) / jnp.sqrt(st_in[j, 1:2, :] + 1e-6)
    gain = (1.0 - beta_two) * (norm_factor * norm_factor)[:, 0:1]
    w_copies[2].wait()
    w_copies[3].wait()
    nl_ref[0] = beta_two * sl[...] + gain * nl_ref[0]
    nr_ref[0] = beta_two * sr[...] + gain * nr_ref[0]

    def dir_wait(k, c):
        j = partner(blk, k, n_blk)
        pltpu.make_async_remote_copy(
            dirs.at[j], ret.at[j], d_send.at[j], d_recv.at[j],
            device_id=(grp, j), device_id_type=MESH,
        ).wait()
        return c

    lax.fori_loop(1, n_blk, dir_wait, 0)
    for b in range(n_tiles):
        s = slot_ref[b]
        up_ref[:, b * block : (b + 1) * block] = (
            ret[s].astype(jnp.float32) * scales[s][:, 0:1]
        ).astype(up_ref.dtype)

    def drain(s, c):
        copy_in(s).wait_send()

        @pl.when(jnp.logical_not(is_end))
        def _():
            copy_out(s).wait_send()

        @pl.when(s != blk)
        def _():
            copy_tile(s).wait_send()

        return c

    lax.fori_loop(0, n_blk, drain, 0)


def shards(n_grp, n_blk, partials, slot_of_block, stat_left, stat_right, root_left, root_right):
    rows, cols = partials.shape[1], partials.shape[2]
    block = stat_left.shape[1]
    n_tiles = cols // block
    vmem = pltpu.VMEM
    dma = pltpu.SemaphoreType.DMA
    half, single = jnp.bfloat16, jnp.float32
    any_spec = pl.BlockSpec(memory_space=pl.ANY)
    vmem_spec = pl.BlockSpec(memory_space=vmem)
    slots = (n_blk, rows, block)
    return pl.pallas_call(
        functools.partial(kernel, n_grp, n_blk),
        out_shape=(
            jax.ShapeDtypeStruct((1, block, block), single),
            jax.ShapeDtypeStruct((1, block, block), single),
            jax.ShapeDtypeStruct((rows, cols), half),
        ),
        in_specs=[pl.BlockSpec(memory_space=pltpu.SMEM)] + [any_spec] * 5,
        out_specs=(vmem_spec,) * 3,
        scratch_shapes=[
            vmem((n_tiles + 1, rows, block), half),
            vmem(slots, half),
            vmem((2, *slots), half),
            vmem(slots, half),
            vmem(slots, half),
            vmem(slots, half),
            vmem((8, 128), single),
            vmem((n_blk, 8, 128), single),
            vmem((n_blk, 1, 128), single),
            vmem((block, block), single),
            vmem((block, block), single),
            vmem((block, block), half),
            vmem((block, block), half),
            dma((n_tiles,)),
            dma((4,)),
            dma((n_blk,)),
            dma((2, n_blk)),
            dma((n_blk,)),
            dma((n_blk,)),
            dma((n_blk,)),
            dma((n_blk,)),
            dma((n_blk,)),
            dma((n_blk,)),
            dma((n_blk,)),
        ],
        compiler_params=pltpu.CompilerParams(collective_id=0, has_side_effects=True),
        name="shampoo",
    )(slot_of_block, partials, stat_left, stat_right, root_left, root_right)


def solution(mesh):
    return jax.shard_map(
        functools.partial(shards, mesh.shape["grp"], mesh.shape["blk"]),
        mesh=mesh,
        in_specs=(
            P("grp", "blk", None),
            P(),
            P("blk", None, None),
            P("blk", None, None),
            P("blk", None, None),
            P("blk", None, None),
        ),
        out_specs=(P("blk", None, None), P("blk", None, None), P("blk", None)),
        check_vma=False,
    )
```

time: 108 us -> 45 us (0.42)
  waiting for transfers between devices: 50.1 us -> 0 us
  Pallas kernels: 0 us -> 39.6 us
  blocking collectives: 15.9 us -> 0 us
  between operations: 16.3 us -> 0.65 us
  starting transfers between devices: 7.45 us -> 0 us
  other arithmetic: 5.64 us -> 0 us
  matrix products: 5.32 us -> 0 us
  local copies, waits for them, and re-layouts: 6.6 us -> 4.45 us
    psum x1 -> x0, waiting for transfers between devices: 42.7 us -> none  [shards(): lax.psum(partials[0].astype(jnp.float32).astype(jnp.bfloat16), 'grp')]
    pallas_call x0 -> x1, Pallas kernels: none -> 39.6 us  [shards(): pl.pallas_call(functools.partial(kernel, n_grp, n_blk), out_shape=(jax.Sh...]
    psum x1 -> x0, blocking collectives: 15.9 us -> none  [shards(): squares = lax.psum(local_sq, 'blk')]
    all_to_all x2 -> x0, starting transfers between devices: 7.41 us -> none  [the longest x1 3.79 us: shards(): lax.all_to_all(jnp.einsum('rbc,bs->src', shaped, selector, preferred_elem...]
    all_to_all x2 -> x0, waiting for transfers between devices: 6.75 us -> none  [the longest x1 6.74 us: shards(): lax.all_to_all(grafted[None], 'blk', split_axis=1, concat_axis=0, tiled=T...]
    dot_general x5 -> x0, matrix products: 5.32 us -> none  [the longest x1 1.6 us: shards(): jnp.dot(halfway, root_right[0], preferred_element_type=jnp.float32)]
    unnamed x1 -> x0, other arithmetic: 3.82 us -> none
    reduce_sum x2 -> x0, other arithmetic: 1.7 us -> none  [the longest x1 0.87 us: shards(): owned_sq = jnp.sum(owned_wide * owned_wide)]
  transfers between devices with their start and end apart: 3 -> 0, of which waited for: 2 -> 0; matrix products, arithmetic and copies ran while one was open for 3% -> 0% of each run, Pallas kernels for 0% -> 0%
where the time goes in v1:
time: 45 us; the launch traced here: 44.7 us
  Pallas kernels  39.6 us (88%)
  local copies, waits for them, and re-layouts  4.45 us (10%)
  between operations  0.65 us (1%)
    pallas_call x1, Pallas kernels, shards(): pl.pallas_call(functools.partial(kernel, n_grp, n_blk), out_shape=(jax.Sh...  39.6 us
    unnamed x7, local copies, waits for them, and re-layouts  4.45 us

profile of v1, /device:TPU:0, one launch (start us, length us, event | category | flops | bytes accessed | tf_op | source)
XLA Modules:
  0.0 44.7 jit_solution(10124840511387808478)
XLA Ops:
  0.6 39.6 %shampoo.1 = (f32[1,512,512]{2,1,0:T(8,128)}, f32[1,512,512]{2,1,0:T(8,128)}, bf16[64,3584]{1,0:T(8,128)(2,1)}) custom-call(s32[7]{0:T(128)} %slot_ref.1, bf16[1,64,3584]{2,1,0:T(8,128)(2,1)} %x_ref.1, f32[1,512,512]{2,1,0:T(8,128)} %sl_ref.1, f32[1,512,512]{2,1,0:T(8,128)} %sr_ref.1, bf16[1,512,512]{2,1,0:T(8,128)(2,1)} %rl_ref.1, bf16[1,512,512]{2,1,0:T(8,128)(2,1)} %rr_ref.1), custom_call_target="tpu_custom_call" | custom-call | tf_op jit(solution)/shard_map/shampoo/pallas_call | solution.py:270
  40.3 0.0 copy-start
  40.3 2.4 %copy.12 = f32[1,512,512]{2,1,0:T(8,128)} copy(f32[1,512,512]{2,1,0:T(8,128)} %get-tuple-element.6) | data formatting | bytes 2097152
  42.7 0.0 copy-done
  42.7 0.0 copy-start.1
  42.7 1.0 %copy.13 = f32[1,512,512]{2,1,0:T(8,128)} copy(f32[1,512,512]{2,1,0:T(8,128)S(1)} %copy-done) | data formatting | bytes 2097152
  43.6 0.4 copy-done.1
  44.0 0.8 %copy.14 = bf16[64,3584]{1,0:T(8,128)(2,1)} copy(bf16[64,3584]{1,0:T(8,128)(2,1)S(1)} %copy-done.1) | data formatting | bytes 917504
Async XLA Ops:
  40.3 2.4 %copy-start = (f32[1,512,512]{2,1,0:T(8,128)S(1)}, f32[1,512,512]{2,1,0:T(8,128)}, u32[]{:S(2)}) copy-start(f32[1,512,512]{2,1,0:T(8,128)} %get-tuple-element.7) | copy-start | bytes 3145732
  42.7 1.3 %copy-start.1 = (bf16[64,3584]{1,0:T(8,128)(2,1)S(1)}, bf16[64,3584]{1,0:T(8,128)(2,1)}, u32[]{:S(2)}) copy-start(bf16[64,3584]{1,0:T(8,128)(2,1)} %get-tuple-element.8) | copy-start | bytes 1376260

commit v2 on v1

--- a/solution.py
+++ b/solution.py
@@ -10,6 +10,7 @@
 
 MESH = pl.DeviceIdType.MESH
 beta_two = 0.9
+vmem_bytes = 67043328
 
 
 def partner(me, k, count):
@@ -257,6 +258,19 @@
     lax.fori_loop(0, n_blk, drain, 0)
 
 
+def writer(*refs):
+    count = len(refs) // 2
+    sources, targets, sems = refs[:count], refs[count:-1], refs[-1]
+    copies = [
+        pltpu.make_async_copy(src, dst, sems.at[i])
+        for i, (src, dst) in enumerate(zip(sources, targets))
+    ]
+    for c in copies:
+        c.start()
+    for c in copies:
+        c.wait()
+
+
 def shards(n_grp, n_blk, partials, slot_of_block, stat_left, stat_right, root_left, root_right):
     rows, cols = partials.shape[1], partials.shape[2]
     block = stat_left.shape[1]
@@ -264,17 +278,19 @@
     vmem = pltpu.VMEM
     dma = pltpu.SemaphoreType.DMA
     half, single = jnp.bfloat16, jnp.float32
-    any_spec = pl.BlockSpec(memory_space=pl.ANY)
+    hbm_spec = pl.BlockSpec(memory_space=pltpu.HBM)
     vmem_spec = pl.BlockSpec(memory_space=vmem)
     slots = (n_blk, rows, block)
-    return pl.pallas_call(
+    results = (
+        ((1, block, block), single),
+        ((1, block, block), single),
+        ((rows, cols), half),
+    )
+    held_bytes = sum(math.prod(shape) * jnp.dtype(dtype).itemsize for shape, dtype in results)
+    held = pl.pallas_call(
         functools.partial(kernel, n_grp, n_blk),
-        out_shape=(
-            jax.ShapeDtypeStruct((1, block, block), single),
-            jax.ShapeDtypeStruct((1, block, block), single),
-            jax.ShapeDtypeStruct((rows, cols), half),
-        ),
-        in_specs=[pl.BlockSpec(memory_space=pltpu.SMEM)] + [any_spec] * 5,
+        out_shape=tuple(vmem(shape, dtype) for shape, dtype in results),
+        in_specs=[pl.BlockSpec(memory_space=pltpu.SMEM)] + [hbm_spec] * 5,
         out_specs=(vmem_spec,) * 3,
         scratch_shapes=[
             vmem((n_tiles + 1, rows, block), half),
@@ -302,9 +318,20 @@
             dma((n_blk,)),
             dma((n_blk,)),
         ],
-        compiler_params=pltpu.CompilerParams(collective_id=0, has_side_effects=True),
+        compiler_params=pltpu.CompilerParams(
+            collective_id=0, has_side_effects=True, vmem_limit_bytes=vmem_bytes - held_bytes
+        ),
         name="shampoo",
     )(slot_of_block, partials, stat_left, stat_right, root_left, root_right)
+    return pl.pallas_call(
+        writer,
+        out_shape=tuple(jax.ShapeDtypeStruct(shape, dtype) for shape, dtype in results),
+        in_specs=[vmem_spec] * 3,
+        out_specs=(hbm_spec,) * 3,
+        scratch_shapes=[dma((3,))],
+        compiler_params=pltpu.CompilerParams(vmem_limit_bytes=2**20),
+        name="writer",
+    )(*held)
 
 
 def solution(mesh):

time: 45 us -> 40.4 us (0.90)
  local copies, waits for them, and re-layouts: 4.45 us -> 0 us
    unnamed x7 -> x0, local copies, waits for them, and re-layouts: 4.45 us -> none
    pallas_call x1 -> x2, Pallas kernels: 39.6 us -> 39.6 us  [the longest x1 38.1 us: shards(): pl.pallas_call(functools.partial(kernel, n_grp, n_blk), out_shape=tuple((...]
where the time goes in v2:
time: 40.4 us; the launch traced here: 40.3 us
  Pallas kernels  39.6 us (98%)
  between operations  0.64 us (2%)
    pallas_call x1, Pallas kernels, shards(): pl.pallas_call(functools.partial(kernel, n_grp, n_blk), out_shape=tuple((...  38.1 us
    pallas_call x1, Pallas kernels, shards(): pl.pallas_call(writer, out_shape=tuple((jax.ShapeDtypeStruct(shape, dtype...  1.49 us

profile of v2, /device:TPU:0, one launch (start us, length us, event | category | flops | bytes accessed | tf_op | source)
XLA Modules:
  0.0 40.3 jit_solution(5070595191115796020)
XLA Ops:
  0.6 38.1 %shampoo.1 = (f32[1,512,512]{2,1,0:T(8,128)S(1)}, f32[1,512,512]{2,1,0:T(8,128)S(1)}, bf16[64,3584]{1,0:T(8,128)(2,1)S(1)}) custom-call(s32[7]{0:T(128)} %slot_ref.1, bf16[1,64,3584]{2,1,0:T(8,128)(2,1)} %x_ref.1, f32[1,512,512]{2,1,0:T(8,128)} %sl_ref.1, f32[1,512,512]{2,1,0:T(8,128)} %sr_ref.1, bf16[1,512,512]{2,1,0:T(8,128)(2,1)} %rl_ref.1, ...), custom_call_target="tpu_custom_call" | custom-call | tf_op jit(solution)/shard_map/shampoo/pallas_call | solution.py:290
  38.8 1.5 %writer.1 = (f32[1,512,512]{2,1,0:T(8,128)}, f32[1,512,512]{2,1,0:T(8,128)}, bf16[64,3584]{1,0:T(8,128)(2,1)}) custom-call(f32[1,512,512]{2,1,0:T(8,128)S(1)} %get-tuple-element.6.refs_0_, f32[1,512,512]{2,1,0:T(8,128)S(1)} %get-tuple-element.7.refs_1_, bf16[64,3584]{1,0:T(8,128)(2,1)S(1)} %get-tuple-element.8.refs_2_), custom_call_target="tpu_custom_call" | custom-call | tf_op jit(solution)/shard_map/writer/pallas_call | solution.py:326

commit v3 on v2

--- a/solution.py
+++ b/solution.py
@@ -30,7 +30,11 @@
 ):
     grp, blk = lax.axis_index("grp"), lax.axis_index("blk")
     n_tiles = xb.shape[0] - 1
-    rows, block = xb.shape[1], xb.shape[2]
+    parts, height, block = xb.shape[1], xb.shape[2], xb.shape[3]
+    rows = parts * height
+    units = n_blk * parts
+    groups = 2 if n_blk % 2 == 0 else 1
+    fellows = n_blk // groups
     half = n_grp // 2
     low = grp < half
     step = jnp.where(low, 1, -1)
@@ -39,18 +43,24 @@
     is_end = depth == half - 1
     inner = grp + step
     outer = jnp.where(is_end, grp, grp - step)
-    lag = jnp.where(is_end, n_blk, jnp.minimum(2 + 3 * depth, n_blk))
-
-    def x_copy(b):
+    lag = jnp.where(is_end, units, jnp.minimum((1 + 2 * depth) * 2 * parts, units))
+    early = jnp.logical_and(is_end, lax.rem(blk, groups) < groups - 1)
+    moment = lag + jnp.where(early, units // groups + 3, units)
+
+    def x_copy(b, h):
         cols = pl.ds(pl.multiple_of(b * block, block), block)
-        return pltpu.make_async_copy(x_ref.at[0, :, cols], xb.at[b], x_sem.at[b])
+        return pltpu.make_async_copy(
+            x_ref.at[0, pl.ds(h * height, height), cols], xb.at[b, h], x_sem.at[b, h]
+        )
 
     def x_start(b, c):
-        x_copy(b).start()
+        for h in range(parts):
+            x_copy(b, h).start()
         return c
 
     def x_wait(b, c):
-        x_copy(b).wait()
+        for h in range(parts):
+            x_copy(b, h).wait()
         return c
 
     lax.fori_loop(0, n_tiles, x_start, 0)
@@ -76,129 +86,139 @@
         pl.semaphore_signal(barrier, inc=1, device_id=(outer, blk), device_id_type=MESH)
 
     lax.fori_loop(1, n_blk, greet, 0)
-    xb[n_tiles] = jnp.zeros((rows, block), xb.dtype)
+    xb[n_tiles] = jnp.zeros((parts, height, block), xb.dtype)
     lax.fori_loop(0, n_tiles, x_wait, 0)
     pl.semaphore_wait(barrier, n_blk + jnp.where(is_end, 0, 1))
 
     kind = jnp.where(is_mid, 1, 0)
 
-    def target(t):
-        return partner(blk, lax.rem(t + 1, n_blk), n_blk)
-
-    def copy_in(s):
-        return pltpu.make_async_remote_copy(
-            snd.at[s], rz.at[kind, s], a_send.at[s], z_recv.at[kind, s],
+    def target(u):
+        k = u // parts
+        fellow = partner(blk // groups, lax.rem(lax.rem(k, fellows) + 1, fellows), fellows)
+        return fellow * groups + k // fellows, lax.rem(u, parts)
+
+    def copy_in(s, h):
+        return pltpu.make_async_remote_copy(
+            snd.at[s, h], rz.at[kind, s, h], a_send.at[s, h], z_recv.at[kind, s, h],
             device_id=(inner, blk), device_id_type=MESH,
         )
 
-    def copy_out(s):
-        return pltpu.make_async_remote_copy(
-            rz.at[1, s], rz.at[1, s], b_send.at[s], z_recv.at[1, s],
+    def copy_out(s, h):
+        return pltpu.make_async_remote_copy(
+            rz.at[1, s, h], rz.at[1, s, h], b_send.at[s, h], z_recv.at[1, s, h],
             device_id=(outer, blk), device_id_type=MESH,
         )
 
-    def arrived(k, s):
-        return pltpu.make_async_remote_copy(
-            rz.at[k, s], rz.at[k, s], a_send.at[s], z_recv.at[k, s],
+    def arrived(k, s, h):
+        return pltpu.make_async_remote_copy(
+            rz.at[k, s, h], rz.at[k, s, h], a_send.at[s, h], z_recv.at[k, s, h],
             device_id=(inner, blk), device_id_type=MESH,
         )
 
-    def copy_tile(s):
-        return pltpu.make_async_remote_copy(
-            rz.at[1, s], tile.at[blk], p_send.at[s], p_recv.at[blk],
+    def copy_tile(s, h):
+        return pltpu.make_async_remote_copy(
+            rz.at[1, s, h], tile.at[blk, h], p_send.at[s, h], p_recv.at[blk, h],
             device_id=(grp, s), device_id_type=MESH,
         )
 
+    def tile_wait(k, c):
+        j = partner(blk, k, n_blk)
+        for h in range(parts):
+            pltpu.make_async_remote_copy(
+                rz.at[1, j, h], tile.at[j, h], p_send.at[j, h], p_recv.at[j, h],
+                device_id=(grp, j), device_id_type=MESH,
+            ).wait_recv()
+        return c
+
+    def copy_dir(j):
+        return pltpu.make_async_remote_copy(
+            dirs.at[j], ret.at[blk], d_send.at[j], d_recv.at[blk],
+            device_id=(grp, j), device_id_type=MESH,
+        )
+
+    def copy_stat(j):
+        return pltpu.make_async_remote_copy(
+            st_out, st_in.at[blk], s_send.at[j], s_recv.at[blk],
+            device_id=(grp, j), device_id_type=MESH,
+        )
+
+    def stat_start(k, c):
+        copy_stat(partner(blk, k, n_blk)).start()
+        return c
+
+    def dir_start(k, c):
+        copy_dir(partner(blk, n_blk - k, n_blk)).start()
+        return c
+
+    def apply():
+        lax.fori_loop(1, n_blk, tile_wait, 0)
+        w_copies[0].wait()
+        w_copies[1].wait()
+        mine = tile[...].reshape(n_blk * rows, block)
+        halfway = jnp.dot(rl[...], mine, preferred_element_type=jnp.float32).astype(jnp.bfloat16)
+        direction = jnp.dot(halfway, rr[...], preferred_element_type=jnp.float32)
+        dirs[...] = direction.astype(dirs.dtype).reshape(n_blk, rows, block)
+        wide = mine.astype(jnp.float32)
+        own_sq = jnp.sum(wide * wide)
+        dir_sq = jnp.sum(direction * direction)
+        row_id = lax.broadcasted_iota(jnp.int32, st_out.shape, 0)
+        stats = jnp.where(row_id == 0, own_sq, dir_sq)
+        st_out[...] = stats
+        st_in[blk] = stats
+        lax.fori_loop(1, n_blk, stat_start, 0)
+        lax.fori_loop(1, n_blk, dir_start, 0)
+        ret[blk] = dirs[blk]
+
     def phase(t, c):
-        @pl.when(t < n_blk)
-        def _():
-            s = target(t)
+        @pl.when(t < units)
+        def _():
+            s, h = target(t)
             b = n_tiles
             for i in range(n_tiles):
                 b = jnp.where(slot_ref[i] == s, i, b)
 
             @pl.when(is_end)
             def _():
-                snd[s] = xb[b]
+                snd[s, h] = xb[b, h]
 
             @pl.when(jnp.logical_not(is_end))
             def _():
-                arrived(0, s).wait_recv()
-                snd[s] = (xb[b].astype(jnp.float32) + rz[0, s].astype(jnp.float32)).astype(snd.dtype)
-
-            copy_in(s).start()
-
-        @pl.when(jnp.logical_and(t >= lag, t < n_blk + lag))
-        def _():
-            s = target(t - lag)
-            arrived(1, s).wait_recv()
+                arrived(0, s, h).wait_recv()
+                total = xb[b, h].astype(jnp.float32) + rz[0, s, h].astype(jnp.float32)
+                snd[s, h] = total.astype(snd.dtype)
+
+            copy_in(s, h).start()
+
+        @pl.when(jnp.logical_and(t >= lag, t < units + lag))
+        def _():
+            s, h = target(t - lag)
+            arrived(1, s, h).wait_recv()
 
             @pl.when(is_mid)
             def _():
-                rz[1, s] = (snd[s].astype(jnp.float32) + rz[1, s].astype(jnp.float32)).astype(rz.dtype)
+                total = snd[s, h].astype(jnp.float32) + rz[1, s, h].astype(jnp.float32)
+                rz[1, s, h] = total.astype(rz.dtype)
 
             @pl.when(jnp.logical_not(is_end))
             def _():
-                copy_out(s).start()
-
-            @pl.when(t - lag < n_blk - 1)
-            def _():
-                copy_tile(s).start()
-
-        return c
-
-    lax.fori_loop(0, 2 * n_blk, phase, 0)
-    tile[blk] = rz[1, blk]
-
-    def tile_wait(k, c):
-        j = partner(blk, k, n_blk)
-        pltpu.make_async_remote_copy(
-            rz.at[1, j], tile.at[j], p_send.at[j], p_recv.at[j],
-            device_id=(grp, j), device_id_type=MESH,
-        ).wait_recv()
-        return c
-
-    lax.fori_loop(1, n_blk, tile_wait, 0)
-    w_copies[0].wait()
-    w_copies[1].wait()
-
+                copy_out(s, h).start()
+
+            @pl.when(s != blk)
+            def _():
+                copy_tile(s, h).start()
+
+            @pl.when(s == blk)
+            def _():
+                tile[blk, h] = rz[1, blk, h]
+
+        @pl.when(t == moment)
+        def _():
+            apply()
+
+        return c
+
+    lax.fori_loop(0, 2 * units + 1, phase, 0)
     owned = tile[...].reshape(n_blk * rows, block)
-    halfway = jnp.dot(rl[...], owned, preferred_element_type=jnp.float32).astype(jnp.bfloat16)
-    direction = jnp.dot(halfway, rr[...], preferred_element_type=jnp.float32)
-    dirs[...] = direction.astype(dirs.dtype).reshape(n_blk, rows, block)
-
-    def copy_dir(j):
-        return pltpu.make_async_remote_copy(
-            dirs.at[j], ret.at[blk], d_send.at[j], d_recv.at[blk],
-            device_id=(grp, j), device_id_type=MESH,
-        )
-
-    def copy_stat(j):
-        return pltpu.make_async_remote_copy(
-            st_out, st_in.at[blk], s_send.at[j], s_recv.at[blk],
-            device_id=(grp, j), device_id_type=MESH,
-        )
-
-    wide = owned.astype(jnp.float32)
-    own_sq = jnp.sum(wide * wide)
-    dir_sq = jnp.sum(direction * direction)
-    row_id = lax.broadcasted_iota(jnp.int32, st_out.shape, 0)
-    stats = jnp.where(row_id == 0, own_sq, dir_sq)
-    st_out[...] = stats
-    st_in[blk] = stats
-
-    def stat_start(k, c):
-        copy_stat(partner(blk, k, n_blk)).start()
-        return c
-
-    def dir_start(k, c):
-        copy_dir(partner(blk, n_blk - k, n_blk)).start()
-        return c
-
-    lax.fori_loop(1, n_blk, stat_start, 0)
-    lax.fori_loop(1, n_blk, dir_start, 0)
-    ret[blk] = dirs[blk]
-
     nl_ref[0] = lax.dot_general(
         owned, owned, (((1,), (1,)), ((), ())), preferred_element_type=jnp.float32
     )
@@ -243,15 +263,18 @@
         ).astype(up_ref.dtype)
 
     def drain(s, c):
-        copy_in(s).wait_send()
+        for h in range(parts):
+            copy_in(s, h).wait_send()
 
         @pl.when(jnp.logical_not(is_end))
         def _():
-            copy_out(s).wait_send()
+            for h in range(parts):
+                copy_out(s, h).wait_send()
 
         @pl.when(s != blk)
         def _():
-            copy_tile(s).wait_send()
+            for h in range(parts):
+                copy_tile(s, h).wait_send()
 
         return c
 
@@ -280,7 +303,9 @@
     half, single = jnp.bfloat16, jnp.float32
     hbm_spec = pl.BlockSpec(memory_space=pltpu.HBM)
     vmem_spec = pl.BlockSpec(memory_space=vmem)
+    parts = 2 if rows % 32 == 0 else 1
     slots = (n_blk, rows, block)
+    pieces = (parts, rows // parts, block)
     results = (
         ((1, block, block), single),
         ((1, block, block), single),
@@ -293,10 +318,10 @@
         in_specs=[pl.BlockSpec(memory_space=pltpu.SMEM)] + [hbm_spec] * 5,
         out_specs=(vmem_spec,) * 3,
         scratch_shapes=[
-            vmem((n_tiles + 1, rows, block), half),
-            vmem(slots, half),
-            vmem((2, *slots), half),
-            vmem(slots, half),
+            vmem((n_tiles + 1, *pieces), half),
+            vmem((n_blk, *pieces), half),
+            vmem((2, n_blk, *pieces), half),
+            vmem((n_blk, *pieces), half),
             vmem(slots, half),
             vmem(slots, half),
             vmem((8, 128), single),
@@ -306,13 +331,13 @@
             vmem((block, block), single),
             vmem((block, block), half),
             vmem((block, block), half),
-            dma((n_tiles,)),
+            dma((n_tiles, parts)),
             dma((4,)),
-            dma((n_blk,)),
-            dma((2, n_blk)),
-            dma((n_blk,)),
-            dma((n_blk,)),
-            dma((n_blk,)),
+            dma((n_blk, parts)),
+            dma((2, n_blk, parts)),
+            dma((n_blk, parts)),
+            dma((n_blk, parts)),
+            dma((n_blk, parts)),
             dma((n_blk,)),
             dma((n_blk,)),
             dma((n_blk,)),

time: 40.4 us -> 39.9 us (0.988)
  Pallas kernels: 39.6 us -> 39 us
    pallas_call x1, Pallas kernels: 38.1 us -> 37.5 us  [shards(): pl.pallas_call(functools.partial(kernel, n_grp, n_blk), out_shape=tuple((...]
where the time goes in v3:
time: 39.9 us; the launch traced here: 39.7 us
  Pallas kernels  39 us (98%)
  between operations  0.64 us (2%)
    pallas_call x1, Pallas kernels, shards(): pl.pallas_call(functools.partial(kernel, n_grp, n_blk), out_shape=tuple((...  37.5 us
    pallas_call x1, Pallas kernels, shards(): pl.pallas_call(writer, out_shape=tuple((jax.ShapeDtypeStruct(shape, dtype...  1.49 us

profile of v3, /device:TPU:0, one launch (start us, length us, event | category | flops | bytes accessed | tf_op | source)
XLA Modules:
  0.0 39.7 jit_solution(13024833521751310078)
XLA Ops:
  0.6 37.5 %shampoo.1 = (f32[1,512,512]{2,1,0:T(8,128)S(1)}, f32[1,512,512]{2,1,0:T(8,128)S(1)}, bf16[64,3584]{1,0:T(8,128)(2,1)S(1)}) custom-call(s32[7]{0:T(128)} %slot_ref.1, bf16[1,64,3584]{2,1,0:T(8,128)(2,1)} %x_ref.1, f32[1,512,512]{2,1,0:T(8,128)} %sl_ref.1, f32[1,512,512]{2,1,0:T(8,128)} %sr_ref.1, bf16[1,512,512]{2,1,0:T(8,128)(2,1)} %rl_ref.1, ...), custom_call_target="tpu_custom_call" | custom-call | tf_op jit(solution)/shard_map/shampoo/pallas_call | solution.py:315
  38.2 1.5 %writer.1 = (f32[1,512,512]{2,1,0:T(8,128)}, f32[1,512,512]{2,1,0:T(8,128)}, bf16[64,3584]{1,0:T(8,128)(2,1)}) custom-call(f32[1,512,512]{2,1,0:T(8,128)S(1)} %get-tuple-element.6.refs_0_, f32[1,512,512]{2,1,0:T(8,128)S(1)} %get-tuple-element.7.refs_1_, bf16[64,3584]{1,0:T(8,128)(2,1)S(1)} %get-tuple-element.8.refs_2_), custom_call_target="tpu_custom_call" | custom-call | tf_op jit(solution)/shard_map/writer/pallas_call | solution.py:351

commit v4 on v3

--- a/solution.py
+++ b/solution.py
@@ -41,11 +41,13 @@
     depth = jnp.where(low, half - 1 - grp, grp - half)
     is_mid = depth == 0
     is_end = depth == half - 1
+    leaf = jnp.logical_and(is_end, half > 1)
+    feeder = jnp.logical_and(depth == half - 2, half > 1)
     inner = grp + step
     outer = jnp.where(is_end, grp, grp - step)
-    lag = jnp.where(is_end, units, jnp.minimum((1 + 2 * depth) * 2 * parts, units))
-    early = jnp.logical_and(is_end, lax.rem(blk, groups) < groups - 1)
-    moment = lag + jnp.where(early, units // groups + 3, units)
+    lag = jnp.minimum((1 + 2 * depth) * 2 * parts, units)
+    early = lax.rem(blk, groups) < groups - 1
+    moment = jnp.where(leaf, units, lag + jnp.where(early, units // groups + 5, units))
 
     def x_copy(b, h):
         cols = pl.ds(pl.multiple_of(b * block, block), block)
@@ -85,10 +87,22 @@
     def _():
         pl.semaphore_signal(barrier, inc=1, device_id=(outer, blk), device_id_type=MESH)
 
+    @pl.when(jnp.logical_or(leaf, feeder))
+    def _():
+        def greet_next(k, c):
+            pl.semaphore_signal(
+                barrier, inc=1, device_id=(jnp.where(leaf, inner, outer), partner(blk, k, n_blk)),
+                device_id_type=MESH,
+            )
+            return c
+
+        lax.fori_loop(1, n_blk, greet_next, 0)
+
     lax.fori_loop(1, n_blk, greet, 0)
     xb[n_tiles] = jnp.zeros((parts, height, block), xb.dtype)
     lax.fori_loop(0, n_tiles, x_wait, 0)
-    pl.semaphore_wait(barrier, n_blk + jnp.where(is_end, 0, 1))
+    next_plane = jnp.where(jnp.logical_or(leaf, feeder), n_blk - 1, 0)
+    pl.semaphore_wait(barrier, n_blk + jnp.where(is_end, 0, 1) + next_plane)
 
     kind = jnp.where(is_mid, 1, 0)
 
@@ -107,6 +121,12 @@
         return pltpu.make_async_remote_copy(
             rz.at[1, s, h], rz.at[1, s, h], b_send.at[s, h], z_recv.at[1, s, h],
             device_id=(outer, blk), device_id_type=MESH,
+        )
+
+    def copy_far(s, h):
+        return pltpu.make_async_remote_copy(
+            rz.at[1, s, h], tile.at[blk, h], b_send.at[s, h], p_recv.at[blk, h],
+            device_id=(outer, s), device_id_type=MESH,
         )
 
     def arrived(k, s, h):
@@ -152,6 +172,11 @@
 
     def apply():
         lax.fori_loop(1, n_blk, tile_wait, 0)
+
+        @pl.when(leaf)
+        def _():
+            tile_wait(0, 0)
+
         w_copies[0].wait()
         w_copies[1].wait()
         mine = tile[...].reshape(n_blk * rows, block)
@@ -189,7 +214,7 @@
 
             copy_in(s, h).start()
 
-        @pl.when(jnp.logical_and(t >= lag, t < units + lag))
+        @pl.when(jnp.logical_and(jnp.logical_not(leaf), jnp.logical_and(t >= lag, t < units + lag)))
         def _():
             s, h = target(t - lag)
             arrived(1, s, h).wait_recv()
@@ -199,7 +224,11 @@
                 total = snd[s, h].astype(jnp.float32) + rz[1, s, h].astype(jnp.float32)
                 rz[1, s, h] = total.astype(rz.dtype)
 
-            @pl.when(jnp.logical_not(is_end))
+            @pl.when(feeder)
+            def _():
+                copy_far(s, h).start()
+
+            @pl.when(jnp.logical_not(jnp.logical_or(is_end, feeder)))
             def _():
                 copy_out(s, h).start()
 
@@ -271,7 +300,7 @@
             for h in range(parts):
                 copy_out(s, h).wait_send()
 
-        @pl.when(s != blk)
+        @pl.when(jnp.logical_and(s != blk, jnp.logical_not(leaf)))
         def _():
             for h in range(parts):
                 copy_tile(s, h).wait_send()

time: 39.9 us -> 35.7 us (0.89)
  Pallas kernels: 39 us -> 34.9 us
    pallas_call x1, Pallas kernels: 37.5 us -> 33.4 us  [shards(): pl.pallas_call(functools.partial(kernel, n_grp, n_blk), out_shape=tuple((...]
where the time goes in v4:
time: 35.7 us; the launch traced here: 35.5 us
  Pallas kernels  34.9 us (98%)
  between operations  0.64 us (2%)
    pallas_call x1, Pallas kernels, shards(): pl.pallas_call(functools.partial(kernel, n_grp, n_blk), out_shape=tuple((...  33.4 us
    pallas_call x1, Pallas kernels, shards(): pl.pallas_call(writer, out_shape=tuple((jax.ShapeDtypeStruct(shape, dtype...  1.49 us

profile of v4, /device:TPU:0, one launch (start us, length us, event | category | flops | bytes accessed | tf_op | source)
XLA Modules:
  0.0 35.5 jit_solution(5023117219249098448)
XLA Ops:
  0.6 33.4 %shampoo.1 = (f32[1,512,512]{2,1,0:T(8,128)S(1)}, f32[1,512,512]{2,1,0:T(8,128)S(1)}, bf16[64,3584]{1,0:T(8,128)(2,1)S(1)}) custom-call(s32[7]{0:T(128)} %slot_ref.1, bf16[1,64,3584]{2,1,0:T(8,128)(2,1)} %x_ref.1, f32[1,512,512]{2,1,0:T(8,128)} %sl_ref.1, f32[1,512,512]{2,1,0:T(8,128)} %sr_ref.1, bf16[1,512,512]{2,1,0:T(8,128)(2,1)} %rl_ref.1, ...), custom_call_target="tpu_custom_call" | custom-call | tf_op jit(solution)/shard_map/shampoo/pallas_call | solution.py:344
  34.0 1.5 %writer.1 = (f32[1,512,512]{2,1,0:T(8,128)}, f32[1,512,512]{2,1,0:T(8,128)}, bf16[64,3584]{1,0:T(8,128)(2,1)}) custom-call(f32[1,512,512]{2,1,0:T(8,128)S(1)} %get-tuple-element.6.refs_0_, f32[1,512,512]{2,1,0:T(8,128)S(1)} %get-tuple-element.7.refs_1_, bf16[64,3584]{1,0:T(8,128)(2,1)S(1)} %get-tuple-element.8.refs_2_), custom_call_target="tpu_custom_call" | custom-call | tf_op jit(solution)/shard_map/writer/pallas_call | solution.py:380

commit v5 on v4

--- a/solution.py
+++ b/solution.py
@@ -46,8 +46,7 @@
     inner = grp + step
     outer = jnp.where(is_end, grp, grp - step)
     lag = jnp.minimum((1 + 2 * depth) * 2 * parts, units)
-    early = lax.rem(blk, groups) < groups - 1
-    moment = jnp.where(leaf, units, lag + jnp.where(early, units // groups + 5, units))
+    moment = jnp.where(leaf, units, lag + units)
 
     def x_copy(b, h):
         cols = pl.ds(pl.multiple_of(b * block, block), block)

time: 35.7 us -> 34.5 us (0.966)
  Pallas kernels: 34.9 us -> 33.7 us
    pallas_call x1, Pallas kernels: 33.4 us -> 32.2 us  [shards(): pl.pallas_call(functools.partial(kernel, n_grp, n_blk), out_shape=tuple((...]
where the time goes in v5:
time: 34.5 us; the launch traced here: 34.3 us
  Pallas kernels  33.7 us (98%)
  between operations  0.64 us (2%)
    pallas_call x1, Pallas kernels, shards(): pl.pallas_call(functools.partial(kernel, n_grp, n_blk), out_shape=tuple((...  32.2 us
    pallas_call x1, Pallas kernels, shards(): pl.pallas_call(writer, out_shape=tuple((jax.ShapeDtypeStruct(shape, dtype...  1.49 us

profile of v5, /device:TPU:0, one launch (start us, length us, event | category | flops | bytes accessed | tf_op | source)
XLA Modules:
  0.0 34.3 jit_solution(5626703715250640395)
XLA Ops:
  0.6 32.2 %shampoo.1 = (f32[1,512,512]{2,1,0:T(8,128)S(1)}, f32[1,512,512]{2,1,0:T(8,128)S(1)}, bf16[64,3584]{1,0:T(8,128)(2,1)S(1)}) custom-call(s32[7]{0:T(128)} %slot_ref.1, bf16[1,64,3584]{2,1,0:T(8,128)(2,1)} %x_ref.1, f32[1,512,512]{2,1,0:T(8,128)} %sl_ref.1, f32[1,512,512]{2,1,0:T(8,128)} %sr_ref.1, bf16[1,512,512]{2,1,0:T(8,128)(2,1)} %rl_ref.1, ...), custom_call_target="tpu_custom_call" | custom-call | tf_op jit(solution)/shard_map/shampoo/pallas_call | solution.py:343
  32.8 1.5 %writer.1 = (f32[1,512,512]{2,1,0:T(8,128)}, f32[1,512,512]{2,1,0:T(8,128)}, bf16[64,3584]{1,0:T(8,128)(2,1)}) custom-call(f32[1,512,512]{2,1,0:T(8,128)S(1)} %get-tuple-element.6.refs_0_, f32[1,512,512]{2,1,0:T(8,128)S(1)} %get-tuple-element.7.refs_1_, bf16[64,3584]{1,0:T(8,128)(2,1)S(1)} %get-tuple-element.8.refs_2_), custom_call_target="tpu_custom_call" | custom-call | tf_op jit(solution)/shard_map/writer/pallas_call | solution.py:379
